TPU v7x, 128 devices: a whole 4x4x4 slice. The times are simulated.
128 devices in a mesh: rowa: 2 (over x_hi), rowb: 16 (over z, y), col: 4 (over x_lo, core).
Axes of the slice: x: 4 (x_hi: 2, x_lo: 2; x = x_hi * 2 + x_lo), y: 4, z: 4, core: 2. Of those that a mesh axis runs over, the one named last changes fastest.
Arguments:
- table: float32 [262144, 512], P(('rowa', 'rowb'), 'col'), may hold values from -12 to 12
- start: float32 [16, 512], P(None, 'col'), may hold values from -6 to 6
Outputs:
- right_vectors: float32 [16, 512], P(None, 'col')
- left_images: float32 [16, 262144], P(None, ('rowa', 'rowb'))
- strengths: float32 [16], replicated
All inputs are finite; a program needn't handle non-finite values.
Results may differ from a plain program's by a relative error of at most 0.00014.
Values sent between devices are 32-bit elements.
A program may use at most 64 MiB of HBM per device.

v0:
```python
import jax
import jax.numpy as jnp
from jax import lax
from jax.sharding import PartitionSpec as P

STEPS = 8
high = lax.Precision.HIGHEST


def joined_along(pieces, dim):
    lengths = list(pieces.shape[1:])
    lengths[dim] *= pieces.shape[0]
    return jnp.moveaxis(pieces, 0, dim).reshape(lengths)


def from_everyone(x, axis):
    length = lax.axis_size(axis)
    return lax.all_to_all(jnp.broadcast_to(x[None], (length, *x.shape)), axis, 0, 0, tiled=True)


def gather_directly(x, axis, dim):
    return joined_along(from_everyone(x, axis), dim)


def apply_rows(vectors, table):
    return lax.dot_general(
        vectors, table, (((1,), (1,)), ((), ())), precision=high, preferred_element_type=jnp.float32
    )


def outer_gram(products):
    return lax.dot_general(
        products,
        products,
        (((1,), (1,)), ((), ())),
        precision=high,
        preferred_element_type=jnp.float32,
    )


def normalize(gram, products):
    lower = jnp.linalg.cholesky(gram)
    return (jax.scipy.linalg.solve_triangular(lower, products, lower=True), lower)


def own_columns(vectors, start):
    width = start.shape[1]
    offset = lax.axis_index("col") * width
    return lax.dynamic_slice_in_dim(vectors, offset, width, 1)


def on_device(table, start):
    regrouped = lax.all_to_all(table, "col", split_axis=0, concat_axis=1, tiled=True)
    rows_total = table.shape[0] * lax.axis_size("rowa") * lax.axis_size("rowb")
    vectors = gather_directly(start, "col", 1)
    partial_cover = lax.dot_general(
        regrouped,
        regrouped,
        (((0,), (0,)), ((), ())),
        precision=high,
        preferred_element_type=jnp.float32,
    )
    cover = lax.psum(partial_cover, ("rowa", "rowb", "col"))
    previous = vectors
    lower = None
    for step in range(STEPS):
        previous = vectors
        products = jnp.dot(vectors, cover, precision=high, preferred_element_type=jnp.float32)
        vectors, lower = normalize(outer_gram(products), products)
    images = apply_rows(previous, regrouped)
    left = gather_directly(images, "col", 1)
    return (own_columns(vectors, start), left, jnp.diagonal(lower) / rows_total)


def solution(mesh):
    placed = (P(("rowa", "rowb"), "col"), P(None, "col"))
    return jax.shard_map(
        on_device,
        mesh=mesh,
        in_specs=placed,
        out_specs=(P(None, "col"), P(None, ("rowa", "rowb")), P()),
        check_vma=False,
    )
```

profile of v0, /device:TPU:1, one launch (start us, length us, event | category | flops | bytes accessed | tf_op | source)
XLA Modules:
  0.0 292.2 jit_solution(9501686616633930515)
XLA Ops:
  7.2 54.2 %all_to_all.29 = f32[4,2048,128]{2,1,0:T(8,128)} all-to-all(f32[4,2048,128]{2,1,0:T(8,128)} %bitcast.136), channel_id=1, replica_groups=mesh['rowa'=2,'rowb'=16,'col'=4] {'col'}, dimensions={0} | all-to-all | bytes 8388608 | tf_op jit(solution)/shard_map/all_to_all | solution.py:53
  61.4 5.4 %copy.40 = f32[2048,4,128]{0,2,1:T(8,128)} copy(f32[2048,4,128]{2,0,1:T(8,128)} %bitcast.135) | data formatting | bytes 8388608 | tf_op jit(solution)/shard_map/all_to_all | solution.py:53
  66.8 10.3 %fusion.51 = f32[512,512]{1,0:T(8,128)} fusion(f32[2048,512]{0,1:T(8,128)} %bitcast.133), kind=kOutput, calls=%fused_computation.81 | convolution fusion | flops 6442450944 | bytes 5242880 | tf_op jit(solution)/shard_map/dot_general | solution.py:56
  77.8 4.3 %all-to-all-start.1 = ((f32[4,16,128]{2,1,0:T(8,128)}), f32[4,16,128]{2,1,0:T(8,128)S(1)}, u32[]{:S(2)}, u32[]{:S(2)}) async-start(f32[4,16,128]{2,1,0:T(8,128)} %broadcast_in_dim.7), calls=%async_computation.1 | async-start | bytes 65536 | tf_op jit(solution)/shard_map/all_to_all | solution.py:18
  82.0 3.2 %all-to-all-done.1 = f32[4,16,128]{2,1,0:T(8,128)S(1)} async-done(((f32[4,16,128]{2,1,0:T(8,128)}), f32[4,16,128]{2,1,0:T(8,128)S(1)}, u32[]{:S(2)}, u32[]{:S(2)}) %all-to-all-start.1) | async-done | bytes 32800 | tf_op jit(solution)/shard_map/all_to_all | solution.py:18
  85.2 143.2 %all-reduce.2.cloned.1.call-done = f32[512,512]{1,0:T(8,128)} async-done(((f32[512,512]{1,0:T(8,128)}), f32[512,512]{1,0:T(8,128)}) %all-reduce.2.cloned.1.call-update) | async-done | bytes 1048592 | tf_op jit(solution)/shard_map/psum | solution.py:63
  228.4 2.0 fusion
  230.6 1.5 cholesky.134
  233.5 1.2 custom-call.14
  234.9 1.9 fusion.53
  237.0 1.5 cholesky.145
  239.8 1.2 custom-call.15
  241.3 1.9 fusion.55
  243.4 1.5 cholesky.156
  246.2 1.2 custom-call.16
  248.5 1.5 cholesky.167
  251.3 1.2 custom-call.17
  253.6 1.5 cholesky.178
  256.4 1.2 custom-call.18
  258.8 1.5 cholesky.189
  263.9 1.5 cholesky.200
  268.2 4.3 %fusion.67 = f32[16,2048]{1,0:T(8,128)S(1)} fusion(f32[16,512]{1,0:T(8,128)S(1)} %fusion.15, f32[2048,512]{0,1:T(8,128)} %bitcast.134), kind=kOutput, calls=%fused_computation.97 | convolution fusion | flops 201326592 | bytes 4358144 | tf_op jit(solution)/shard_map/dot_general | solution.py:26
  273.3 3.5 %all-to-all-start.2 = ((f32[4,16,2048]{2,1,0:T(8,128)}), f32[4,16,2048]{2,1,0:T(8,128)S(1)}, u32[]{:S(2)}, u32[]{:S(2)}) async-start(f32[4,16,2048]{2,1,0:T(8,128)} %broadcast_in_dim.8), calls=%async_computation.2 | async-start | bytes 1048576 | tf_op jit(solution)/shard_map/all_to_all | solution.py:18
  277.6 1.5 cholesky.211
  (78 shorter events, 26.1 us)
Async XLA Ops:
  7.2 221.3 %all-reduce.2.cloned.1.call-start = ((), (), s32[]{:S(2)}) async-start(), calls=%async_computation.3 | async-start | bytes 2097152 | tf_op jit(solution)/shard_map/psum | solution.py:63
  66.8 10.3 %copy-start.1 = (f32[16,128]{1,0:T(8,128)S(1)}, f32[16,128]{1,0:T(8,128)}, u32[]{:S(2)}) copy-start(f32[16,128]{1,0:T(8,128)} %param.6) | copy-start | bytes 24580
  77.8 7.4 %all-to-all-start.1 = ((f32[4,16,128]{2,1,0:T(8,128)}), f32[4,16,128]{2,1,0:T(8,128)S(1)}, u32[]{:S(2)}, u32[]{:S(2)}) async-start(f32[4,16,128]{2,1,0:T(8,128)} %broadcast_in_dim.7), calls=%async_computation.1 | async-start | bytes 65536 | tf_op jit(solution)/shard_map/all_to_all | solution.py:18
  228.4 19.2 %copy-start = (f32[512,512]{1,0:T(8,128)S(1)}, f32[512,512]{1,0:T(8,128)}, u32[]{:S(2)}) copy-start(f32[512,512]{1,0:T(8,128)} %all-reduce.2.cloned.1.call-done) | copy-start | bytes 3145732
  273.3 11.2 %all-to-all-start.2 = ((f32[4,16,2048]{2,1,0:T(8,128)}), f32[4,16,2048]{2,1,0:T(8,128)S(1)}, u32[]{:S(2)}, u32[]{:S(2)}) async-start(f32[4,16,2048]{2,1,0:T(8,128)} %broadcast_in_dim.8), calls=%async_computation.2 | async-start | bytes 1048576 | tf_op jit(solution)/shard_map/all_to_all | solution.py:18
Sparse Core Ops, SparseCore 0:
  77.2 151.1 all-reduce.1
where the time goes:
time: 293 us; the launch traced here: 292 us
  waiting for transfers between devices  147 us (50%)
  blocking collectives  54.2 us (18%)
  other arithmetic  32.8 us (11%)
  matrix products  26.4 us (9%)
  between operations  14.2 us (5%)
  local copies, waits for them, and re-layouts  9.6 us (3%)
  starting transfers between devices  7.77 us (3%)
    psum x1, waiting for transfers between devices, on_device(): cover = lax.psum(partial_cover, ('rowa', 'rowb', 'col'))  143 us
    all_to_all x1, blocking collectives, on_device(): lax.all_to_all(table, 'col', split_axis=0, concat_axis=1, tiled=True)  54.2 us
    another operation x24, other arithmetic, normalize(): lower = jnp.linalg.cholesky(gram)  17.2 us
    another operation x16, other arithmetic, normalize(): jax.scipy.linalg.solve_triangular(lower, products, lower=True)  15 us
    dot_general x1, matrix products, on_device(): lax.dot_general(regrouped, regrouped, (((0,), (0,)), ((), ())), precision...  10.3 us
    dot_general x8, matrix products, on_device(): jnp.dot(vectors, cover, precision=high, preferred_element_type=jnp.float32)  8.81 us
    all_to_all x2, starting transfers between devices, from_everyone(): lax.all_to_all(jnp.broadcast_to(x[None], (length, *x.shape)), axis, 0, 0,...  7.73 us
  transfers between devices with their start and end apart: 3, of which 3 were waited for; matrix products, arithmetic and copies ran while one was open for 3% of the time, Pallas kernels for 0%

commit v1 on v0

--- a/solution.py
+++ b/solution.py
@@ -50,7 +50,10 @@
 
 
 def on_device(table, start):
-    regrouped = lax.all_to_all(table, "col", split_axis=0, concat_axis=1, tiled=True)
+    regrouped = jnp.concatenate(
+        lax.all_to_all(jnp.stack(jnp.split(table, lax.axis_size("col"), axis=0)), "col", 0, 0),
+        axis=1,
+    )
     rows_total = table.shape[0] * lax.axis_size("rowa") * lax.axis_size("rowb")
     vectors = gather_directly(start, "col", 1)
     partial_cover = lax.dot_general(

time: 293 us -> 295 us (level)
  local copies, waits for them, and re-layouts: 9.6 us -> 15.8 us
  blocking collectives: 54.2 us -> 51.2 us
    unnamed x4 -> x10, local copies, waits for them, and re-layouts: 0.02 us -> 7.75 us
    all_to_all x1 -> x0, local copies, waits for them, and re-layouts: 5.37 us -> none  [on_device(): lax.all_to_all(table, 'col', split_axis=0, concat_axis=1, tiled=True)]
    split x0 -> x1, local copies, waits for them, and re-layouts: none -> 3.84 us  [on_device(): jnp.split(table, lax.axis_size('col'), axis=0)]
    all_to_all x1, blocking collectives: 54.2 us -> 51.2 us  [on_device(): lax.all_to_all(jnp.stack(jnp.split(table, lax.axis_size('col'), axis=0)),...]
where the time goes in v1:
time: 295 us
  waiting for transfers between devices  147 us (50%)
  blocking collectives  51.2 us (17%)
  other arithmetic  34.7 us (12%)
  matrix products  24 us (8%)
  local copies, waits for them, and re-layouts  15.8 us (5%)
  between operations  14.2 us (5%)
  starting transfers between devices  7.77 us (3%)
    psum x1, waiting for transfers between devices, on_device(): cover = lax.psum(partial_cover, ('rowa', 'rowb', 'col'))  143 us
    all_to_all x1, blocking collectives, on_device(): lax.all_to_all(jnp.stack(jnp.split(table, lax.axis_size('col'), axis=0)),...  51.2 us
    another operation x24, other arithmetic, normalize(): lower = jnp.linalg.cholesky(gram)  17.2 us
    another operation x16, other arithmetic, normalize(): jax.scipy.linalg.solve_triangular(lower, products, lower=True)  15 us
    dot_general x8, matrix products, on_device(): jnp.dot(vectors, cover, precision=high, preferred_element_type=jnp.float32)  8.82 us
    dot_general x1, matrix products, on_device(): lax.dot_general(regrouped, regrouped, (((0,), (0,)), ((), ())), precision...  7.93 us
    unnamed x10, local copies, waits for them, and re-layouts  7.75 us
    all_to_all x2, starting transfers between devices, from_everyone(): lax.all_to_all(jnp.broadcast_to(x[None], (length, *x.shape)), axis, 0, 0,...  7.74 us
  transfers between devices with their start and end apart: 3, of which 3 were waited for; matrix products, arithmetic and copies ran while one was open for 3% of the time, Pallas kernels for 0%

profile of v1, /device:TPU:1, one launch (start us, length us, event | category | flops | bytes accessed | tf_op | source)
XLA Modules:
  0.0 294.7 jit_solution(7297188911827227322)
XLA Ops:
  7.2 3.8 %fusion.51 = (f32[2048,128]{1,0:T(8,128)S(1)}, f32[2048,128]{1,0:T(8,128)}, f32[2048,128]{1,0:T(8,128)}, f32[2048,128]{1,0:T(8,128)S(1)}) fusion(f32[8192,128]{1,0:T(8,128)} %param.5), kind=kLoop, calls=%fused_computation.82 | loop fusion | bytes 8388608 | tf_op jit(solution)/shard_map/split | solution.py:54
  11.4 1.6 copy.53
  13.0 2.6 copy.54
  15.5 1.3 copy.55
  16.9 1.8 pad_maximum_fusion
  18.7 51.2 %all_to_all.15 = f32[4,2048,128]{1,2,0:T(8,128)S(1)} all-to-all(f32[4,2048,128]{1,2,0:T(8,128)S(1)} %pad_maximum_fusion), channel_id=1, replica_groups=mesh['rowa'=2,'rowb'=16,'col'=4] {'col'}, dimensions={0} | all-to-all | bytes 8388608 | tf_op jit(solution)/shard_map/all_to_all | solution.py:54
  69.9 1.9 copy-done
  71.8 7.9 %fusion.52 = f32[512,512]{1,0:T(8,128)} fusion(f32[2048,512]{0,1:T(8,128)S(1)} %bitcast.137), kind=kOutput, calls=%fused_computation.83 | convolution fusion | flops 6442450944 | bytes 5242880 | tf_op jit(solution)/shard_map/dot_general | solution.py:59
  80.4 4.3 %all-to-all-start.1 = ((f32[4,16,128]{2,1,0:T(8,128)}), f32[4,16,128]{2,1,0:T(8,128)S(1)}, u32[]{:S(2)}, u32[]{:S(2)}) async-start(f32[4,16,128]{2,1,0:T(8,128)} %broadcast_in_dim.7), calls=%async_computation.1 | async-start | bytes 65536 | tf_op jit(solution)/shard_map/all_to_all | solution.py:18
  84.7 3.2 %all-to-all-done.1 = f32[4,16,128]{2,1,0:T(8,128)S(1)} async-done(((f32[4,16,128]{2,1,0:T(8,128)}), f32[4,16,128]{2,1,0:T(8,128)S(1)}, u32[]{:S(2)}, u32[]{:S(2)}) %all-to-all-start.1) | async-done | bytes 32800 | tf_op jit(solution)/shard_map/all_to_all | solution.py:18
  87.8 143.1 %all-reduce.2.cloned.1.call-done = f32[512,512]{1,0:T(8,128)} async-done(((f32[512,512]{1,0:T(8,128)}), f32[512,512]{1,0:T(8,128)}) %all-reduce.2.cloned.1.call-update) | async-done | bytes 1048592 | tf_op jit(solution)/shard_map/psum | solution.py:66
  231.0 2.0 fusion
  233.2 1.5 cholesky.134
  237.4 1.9 fusion.54
  239.5 1.5 cholesky.145
  243.8 1.9 fusion.56
  245.9 1.5 cholesky.156
  251.0 1.5 cholesky.167
  256.2 1.5 cholesky.178
  261.3 1.5 cholesky.189
  266.4 1.5 cholesky.200
  270.7 4.3 %fusion.68 = f32[16,2048]{1,0:T(8,128)S(1)} fusion(f32[16,512]{1,0:T(8,128)S(1)} %fusion.15, f32[2048,512]{0,1:T(8,128)} %bitcast.138), kind=kOutput, calls=%fused_computation.99 | convolution fusion | flops 201326592 | bytes 4358144 | tf_op jit(solution)/shard_map/dot_general | solution.py:26
  275.8 3.5 %all-to-all-start.2 = ((f32[4,16,2048]{2,1,0:T(8,128)}), f32[4,16,2048]{2,1,0:T(8,128)S(1)}, u32[]{:S(2)}, u32[]{:S(2)}) async-start(f32[4,16,2048]{2,1,0:T(8,128)} %broadcast_in_dim.8), calls=%async_computation.2 | async-start | bytes 1048576 | tf_op jit(solution)/shard_map/all_to_all | solution.py:18
  280.1 1.5 cholesky.211
  (85 shorter events, 32.5 us)
Async XLA Ops:
  7.2 223.8 %all-reduce.2.cloned.1.call-start = ((), (), s32[]{:S(2)}) async-start(), calls=%async_computation.3 | async-start | bytes 2097152 | tf_op jit(solution)/shard_map/psum | solution.py:66
  69.9 1.9 copy-start
  71.8 8.0 %copy-start.2 = (f32[16,128]{1,0:T(8,128)S(1)}, f32[16,128]{1,0:T(8,128)}, u32[]{:S(2)}) copy-start(f32[16,128]{1,0:T(8,128)} %param.6) | copy-start | bytes 24580
  80.4 7.5 %all-to-all-start.1 = ((f32[4,16,128]{2,1,0:T(8,128)}), f32[4,16,128]{2,1,0:T(8,128)S(1)}, u32[]{:S(2)}, u32[]{:S(2)}) async-start(f32[4,16,128]{2,1,0:T(8,128)} %broadcast_in_dim.7), calls=%async_computation.1 | async-start | bytes 65536 | tf_op jit(solution)/shard_map/all_to_all | solution.py:18
  231.0 19.2 %copy-start.1 = (f32[512,512]{1,0:T(8,128)S(1)}, f32[512,512]{1,0:T(8,128)}, u32[]{:S(2)}) copy-start(f32[512,512]{1,0:T(8,128)} %all-reduce.2.cloned.1.call-done) | copy-start | bytes 3145732
  275.8 11.2 %all-to-all-start.2 = ((f32[4,16,2048]{2,1,0:T(8,128)}), f32[4,16,2048]{2,1,0:T(8,128)S(1)}, u32[]{:S(2)}, u32[]{:S(2)}) async-start(f32[4,16,2048]{2,1,0:T(8,128)} %broadcast_in_dim.8), calls=%async_computation.2 | async-start | bytes 1048576 | tf_op jit(solution)/shard_map/all_to_all | solution.py:18
Sparse Core Ops, SparseCore 0:
  79.9 151.0 all-reduce.1
